TPU v7x, 32 devices: a whole 2x2x4 slice. The times are simulated.
32 devices in a mesh: band: 8 (over z, x), patch: 4 (over y, core).
Axes of the slice: x: 2, y: 2, z: 4, core: 2. Of those that a mesh axis runs over, the one named last changes fastest.
Arguments:
- latents: bfloat16 [8, 10240, 512], P('band', 'patch'), may hold values from -6 to 6
- owners: int32 [16], replicated, may hold values from 0 to 3, as said below
- block_rows: int32 [16, 128], replicated, may hold values from 0 to 2559
- interp_weights: bfloat16 [16, 1024, 128], P('band', 'patch'), may hold values from -0.5 to 0.5
- w_first: bfloat16 [8, 512, 512], P('band'), may hold values from -0.25 to 0.25
- b_first: float32 [8, 512], P('band'), may hold values from -3 to 3
- w_second: bfloat16 [8, 512, 512], P('band'), may hold values from -0.25 to 0.25
- b_second: float32 [8, 512], P('band'), may hold values from -4 to 4
- gain: float32 [8, 512], P('band'), may hold values from 0.1 to 1.9
- w_out: bfloat16 [8, 12, 512], P('band'), may hold values from -0.25 to 0.25
- b_out: float32 [8, 12], P('band'), may hold values from -4 to 4
Outputs:
- grid_fields: float32 [8, 12, 16384], P('band', None, 'patch')
Inputs may be any that keep to these rules, and one draw needn't show every extreme that they name: `owners`: no patch owns more than 8 tiles, and one patch owns exactly 8.
All inputs are finite; a program needn't handle non-finite values.
Results may differ from a plain program's by a relative error of at most 0.003.
Values may be sent and summed in bfloat16 or wider, within the bound.
A program may use at most 64 MiB of HBM per device.

v0:
```python
import functools

import jax
import jax.numpy as jnp
from jax import lax
from jax.experimental import pallas as pl
from jax.experimental.pallas import tpu as pltpu
from jax.sharding import PartitionSpec as P

LEAD = 2


def kernel(
    nb, np_, tiles, blk, cl,
    owners, rows, w_b1, w_b2, w_gain, w_out, w_bo, latents, pieces, w_first, w_second,
    out,
    lat, w1, w2, perm, onehot, acc, sib, own, from_sib, from_chip, weights, block,
    lat_sem, wt_sem, piece_send, w_recv, w_send, sib_send, sib_recv, chip_send, chip_recv,
):
    b, p = lax.axis_index("band"), lax.axis_index("patch")
    n_chips = np_ // 2
    tb, tp = tiles // nb, tiles // np_
    g = tp // tb
    n_z = nb // 2
    q, c = p // 2, p % 2
    z, x = b // 2, b % 2
    units = g * tb * n_chips
    rows_u = 2 * cl
    mesh_dev, width = latents.shape
    depth = onehot.shape[1]
    mesh_type = pl.DeviceIdType.MESH

    def dev(band, patch):
        return {"band": band, "patch": patch}

    def remote(src, dst, send, recv, band, patch):
        return pltpu.make_async_remote_copy(
            src_ref=src, dst_ref=dst, send_sem=send, recv_sem=recv,
            device_id=dev(band, patch), device_id_type=mesh_type,
        )

    barrier = pltpu.get_barrier_semaphore()

    def greet(band, patch):
        pl.semaphore_signal(barrier, inc=1, device_id=dev(band, patch), device_id_type=mesh_type)

    for d in range(1, np_):
        greet(b, (p + d) % np_)
    greet(2 * z + 1 - x, p)

    @pl.when(z > 0)
    def _():
        greet(b - 2, p)

    @pl.when(z < n_z - 1)
    def _():
        greet(b + 2, p)

    lat_copies = [
        pltpu.make_async_copy(
            latents.at[pl.ds(k * depth, depth)], lat.at[pl.ds(k * depth, depth)], lat_sem.at[k]
        )
        for k in range(mesh_dev // depth)
    ]
    for copy in lat_copies:
        copy.start()
    w1_copy = pltpu.make_async_copy(w_first, w1, wt_sem.at[0])
    w2_copy = pltpu.make_async_copy(w_second, w2, wt_sem.at[1])
    w1_copy.start()
    w2_copy.start()

    offsets = list(range(1, n_chips)) + [0]
    order = []
    for d_list in (offsets[:-1], offsets[-1:]):
        for core in (1 - c, c):
            for d in d_list:
                for i in range(tp):
                    order.append((2 * ((q + d) % n_chips) + core) * tp + i)
    perm[...] = jnp.full(perm.shape, -1, jnp.int32)
    for k, t in enumerate(order):
        mine = (owners[t] == p).astype(jnp.int32)
        perm[k : k + 1, :] = rows[pl.ds(t, 1), :] * mine + (mine - 1)
    columns = perm[...].T

    pl.semaphore_wait(barrier, np_ + (z > 0).astype(jnp.int32) + (z < n_z - 1).astype(jnp.int32))

    home = b // g
    own_source = b % g
    piece_copies = [
        (
            pieces.at[i],
            weights.at[own_source * tb + i, pl.ds(pl.multiple_of(p * cl, cl), cl)],
            w_recv.at[own_source, i, p],
            piece_send.at[i],
        )
        for i in range(tb)
    ]

    @pl.when(p == home)
    def _():
        for src, dst, recv, _ in piece_copies:
            pltpu.make_async_copy(src, dst, recv).start()

    @pl.when(p != home)
    def _():
        for src, dst, recv, send in piece_copies:
            remote(src, dst, send, recv, b, home).start()

    def unit_of(n):
        jj, k = n % g, n // g
        i, dd = k // n_chips, k % n_chips
        j = (x + jj) % g
        qq = (q + dd) % n_chips
        return i, j, qq

    def piece(n, half):
        i, j, qq = unit_of(n)
        at = qq * 2 + half
        part = weights.at[j * tb + i, pl.ds(pl.multiple_of(at * cl, cl), cl)]
        return part, w_recv.at[j, i, at]

    def line_of(n):
        source = p * g + unit_of(n)[1]
        return source // 2, x == source % 2

    def forwards(n, half, act):
        zs, on_line = line_of(n)
        part, recv = piece(n, half)
        slot = 2 * n + half

        @pl.when(on_line & (z >= zs) & (z < n_z - 1))
        def _():
            act(remote(part, part, w_send.at[0, slot], recv, b + 2, p))

        @pl.when(on_line & (z <= zs) & (z > 0))
        def _():
            act(remote(part, part, w_send.at[1, slot], recv, b - 2, p))

        @pl.when(on_line)
        def _():
            act(remote(part, part, w_send.at[2, slot], recv, 2 * z + 1 - x, p))

    def arrive(n, half):
        part, recv = piece(n, half)
        pltpu.make_async_copy(part, part, recv).wait()

    def relay(n, at_source):
        zs, on_line = line_of(n)

        @pl.when(on_line & ((z == zs) if at_source else (z != zs)))
        def _():
            for half in range(2):
                arrive(n, half)
                forwards(n, half, lambda copy: copy.start())

    def relay_range(first, last):
        lax.fori_loop(first, last, lambda n, carry: (relay(n, True), carry)[1], 0)

    iota = lax.broadcasted_iota(jnp.int32, (blk, depth), 1)

    def gather(first, count, dst, first_time):
        for k in range(mesh_dev // depth):
            if first_time:
                lat_copies[k].wait()
            for r in range(count):
                hit = iota == (columns[:, first + r : first + r + 1] - k * depth)
                onehot[r * blk : (r + 1) * blk, :] = jnp.where(hit, 1.0, 0.0).astype(jnp.bfloat16)
            part = jnp.dot(
                onehot[: count * blk, :], lat[k * depth : (k + 1) * depth, :],
                preferred_element_type=jnp.float32,
            )
            if k:
                part = part + acc[: count * blk, :]
            if k < mesh_dev // depth - 1:
                acc[: count * blk, :] = part
            else:
                dst[...] = part.astype(jnp.bfloat16).reshape(dst.shape)

    def to_sibling(d, i):
        return remote(
            sib.at[d, i], from_sib.at[d, i], sib_send.at[d, i], sib_recv.at[d, i], b, 2 * q + 1 - c
        )

    def to_chip(d, i):
        return remote(
            own.at[d, i], from_chip.at[d - 1, i], chip_send.at[d - 1, i], chip_recv.at[d - 1, i],
            b, 2 * ((q + d) % n_chips) + c,
        )

    far = (n_chips - 1) * tp
    cut = [units // 4, units // 2, units] if n_chips > 1 else [0, 0, units]
    if n_chips > 1:
        gather(0, far, sib.at[pl.ds(1, n_chips - 1)], True)
        for d in range(1, n_chips):
            for i in range(tp):
                to_sibling(d, i).start()
        relay_range(0, cut[0])
        gather(far, far, own.at[pl.ds(1, n_chips - 1)], False)
        for i in range(tb):
            for jj in range(g):
                it = ((x + jj) % g) * tb + i
                for d in range(1, n_chips):
                    to_sibling(d, it).wait_recv()
                    own[d, it] = own[d, it] + from_sib[d, it]
                    to_chip(d, it).start()
    relay_range(cut[0], cut[1])
    gather(2 * far, tp, sib.at[pl.ds(0, 1)], n_chips == 1)
    for i in range(tp):
        to_sibling(0, i).start()
    relay_range(cut[1], cut[2])
    gather(2 * far + tp, tp, own.at[pl.ds(0, 1)], False)

    w1_copy.wait()
    w2_copy.wait()
    for n in range(min(LEAD, units)):
        relay(n, False)

    channels = w_bo.shape[1]
    eye = lax.broadcasted_iota(jnp.int32, (channels, channels), 0) == lax.broadcasted_iota(
        jnp.int32, (channels, channels), 1
    )
    bias = jnp.sum(jnp.where(eye, w_bo[...], 0.0), axis=1, keepdims=True)

    def decode(n, carry):
        @pl.when(n + LEAD < units)
        def _():
            relay(n + LEAD, False)

        @pl.when(jnp.logical_not(line_of(n)[1]))
        def _():
            for half in range(2):
                arrive(n, half)

        i, j, qq = unit_of(n)
        tile = j * tb + i

        @pl.when((n // g) % n_chips == 0)
        def _():
            to_sibling(0, tile).wait_recv()
            total = own[0, tile] + from_sib[0, tile]
            for d in range(1, n_chips):
                to_chip(d, tile).wait_recv()
                total = total + from_chip[d - 1, tile]
            block[tile] = total

        start = pl.multiple_of(qq * rows_u, rows_u)
        interp = jnp.dot(
            weights[tile, pl.ds(start, rows_u), :], block[tile], preferred_element_type=jnp.float32
        ).astype(jnp.bfloat16)
        v = jnp.dot(interp, w1[...], preferred_element_type=jnp.float32) + w_b1[...]
        half = 0.5 * v
        hidden = (half * jnp.tanh(half) + half).astype(jnp.bfloat16)
        second = jnp.dot(hidden, w2[...], preferred_element_type=jnp.float32) + w_b2[...]
        centred = second - jnp.mean(second, axis=-1, keepdims=True)
        variance = jnp.mean(centred * centred, axis=-1, keepdims=True)
        normed = (centred * lax.rsqrt(variance + 1e-05) * w_gain[...]).astype(jnp.bfloat16)
        result = lax.dot_general(
            w_out[...], normed, (((1,), (1,)), ((), ())), preferred_element_type=jnp.float32
        )
        at = pl.multiple_of(tile * (np_ * cl) + start, rows_u)
        result = result + bias
        for ch in range(channels):
            out[ch, :, pl.ds(at, rows_u)] = result[ch : ch + 1]
        return carry

    lax.fori_loop(0, units, decode, 0)

    @pl.when(p != home)
    def _():
        for src, dst, recv, send in piece_copies:
            remote(src, dst, send, recv, b, home).wait_send()

    for d in range(n_chips):
        for i in range(tp):
            to_sibling(d, i).wait_send()
            if d:
                to_chip(d, i).wait_send()

    def drain(n, carry):
        for half in range(2):
            forwards(n, half, lambda copy: copy.wait_send())
        return carry

    lax.fori_loop(0, units, drain, 0)


def solution(mesh):
    nb, np_ = mesh.shape["band"], mesh.shape["patch"]

    def body(
        latents, owners, block_rows, pieces, w_first, b_first, w_second, b_second, gain, w_out, b_out
    ):
        tiles, blk = block_rows.shape
        cl, channels = pieces.shape[1], w_out.shape[1]
        mesh_dev, width = latents.shape[1:]
        n_chips, tb, tp = np_ // 2, tiles // nb, tiles // np_
        g = tp // tb
        units = g * tb * n_chips
        depth = next(k for k in (512, 256, 128, mesh_dev) if mesh_dev % k == 0)
        group = max(n_chips - 1, 1) * tp * blk
        vmem = pl.BlockSpec(memory_space=pltpu.VMEM)
        hbm = pl.BlockSpec(memory_space=pl.ANY)
        bf16 = jnp.bfloat16
        dma = pltpu.SemaphoreType.DMA
        result = pl.pallas_call(
            functools.partial(kernel, nb, np_, tiles, blk, cl),
            out_shape=jax.ShapeDtypeStruct((channels, 1, tp * np_ * cl), jnp.float32),
            in_specs=[pl.BlockSpec(memory_space=pltpu.SMEM)] + [vmem] * 6 + [hbm] * 4,
            out_specs=vmem,
            scratch_shapes=[
                pltpu.VMEM((mesh_dev, width), bf16),
                pltpu.VMEM(w_first.shape[1:], bf16),
                pltpu.VMEM(w_second.shape[1:], bf16),
                pltpu.VMEM((blk, blk), jnp.int32),
                pltpu.VMEM((group, depth), bf16),
                pltpu.VMEM((group, width), jnp.float32),
                pltpu.VMEM((n_chips, tp, blk, width), bf16),
                pltpu.VMEM((n_chips, tp, blk, width), bf16),
                pltpu.VMEM((n_chips, tp, blk, width), bf16),
                pltpu.VMEM((max(n_chips - 1, 1), tp, blk, width), bf16),
                pltpu.VMEM((tp, np_ * cl, blk), bf16),
                pltpu.VMEM((tp, blk, width), bf16),
                dma((mesh_dev // depth,)),
                dma((2,)),
                dma((tb,)),
                dma((g, tb, np_)),
                dma((3, 2 * units)),
                dma((n_chips, tp)),
                dma((n_chips, tp)),
                dma((max(n_chips - 1, 1), tp)),
                dma((max(n_chips - 1, 1), tp)),
            ],
            compiler_params=pltpu.CompilerParams(collective_id=0, has_side_effects=True),
            name="decode",
        )(
            owners, block_rows, b_first, b_second, gain, w_out[0], b_out,
            latents[0], pieces, w_first[0], w_second[0],
        )
        return jnp.transpose(result, (1, 0, 2))

    return jax.shard_map(
        body,
        mesh=mesh,
        in_specs=(
            P("band", "patch", None),
            P(),
            P(),
            P("band", "patch", None),
            P("band", None, None),
            P("band", None),
            P("band", None, None),
            P("band", None),
            P("band", None),
            P("band", None, None),
            P("band", None),
        ),
        out_specs=P("band", None, "patch"),
        check_vma=False,
    )
```

profile of v0, /device:TPU:5, one launch (start us, length us, event | category | flops | bytes accessed | tf_op | source)
XLA Modules:
  0.0 36.3 jit_solution(1808586068534667682)
XLA Ops:
  0.0 34.7 %decode.1 = f32[12,1,4096]{2,1,0:T(1,128)} custom-call(s32[16]{0:T(128)} %owners.1, s32[16,128]{1,0:T(8,128)} %rows.1, f32[1,512]{1,0:T(1,128)} %w_b1.1, f32[1,512]{1,0:T(1,128)} %w_b2.1, f32[1,512]{1,0:T(1,128)} %w_gain.1, bf16[12,512]{1,0:T(8,128)(2,1)} %bitcast.9, f32[1,12]{1,0:T(1,128)} %w_bo.1, bf16[2560,512]{1,0:T(8,128)(2,1)} %bitcast.5, ...), custom_call_target="tpu_custom_call" | custom-call | tf_op jit(solution)/shard_map/decode/pallas_call | solution.py:305
  34.7 1.6 %copy.13 = f32[1,12,4096]{2,0,1:T(1,128)} copy(f32[1,12,4096]{2,0,1:T(1,128)} %bitcast.6) | data formatting | bytes 393216
where the time goes:
time: 36.5 us; the launch traced here: 36.3 us
  Pallas kernels  34.7 us (95%)
  local copies, waits for them, and re-layouts  1.62 us (4%)
    pallas_call x1, Pallas kernels, body(): pl.pallas_call(functools.partial(kernel, nb, np_, tiles, blk, cl), out_sh...  34.7 us
    unnamed x1, local copies, waits for them, and re-layouts  1.62 us

commit v1 on v0

v1 whole, which is shorter than its diff:
```python
import functools

import jax
import jax.numpy as jnp
from jax import lax
from jax.experimental import pallas as pl
from jax.experimental.pallas import tpu as pltpu
from jax.sharding import PartitionSpec as P

EXT = 32
PARTS = 2


def contract_last(a, b):
    return lax.dot_general(a, b, (((1,), (1,)), ((), ())), preferred_element_type=jnp.float32)


def split(value):
    high = value.astype(jnp.bfloat16)
    return high, value - high.astype(jnp.float32)


def when(condition, action):
    if condition is True:
        action()
    elif condition is not False:
        pl.when(condition)(action)


def kernel(
    nb, np_, tiles, blk, cl, slots,
    owners, rows, w_b1, w_b2, w_gain, w_out, w_bo, latents, pieces, w_first, w_second,
    out,
    lat, w1, w2, mine, perm, onehot, own0, own1, sib0, sib1, far, from_chip, weights,
    w1t, w2e, b2b, bft, rank_of,
    lat_sem, wt_sem, mine_sem, piece_send, w_recv, z_send, x_send,
    sib_send, sib_recv, chip_send, chip_recv,
):
    b, p = lax.axis_index("band"), lax.axis_index("patch")
    n_chips = np_ // 2
    tb, tp = tiles // nb, tiles // np_
    g = tp // tb
    n_z = nb // 2
    q, c = p // 2, p % 2
    z, x = b // 2, b % 2
    mesh_dev, width = latents.shape
    wide = width // 2
    rows_u = 2 * cl
    channels = w_bo.shape[1]
    bf16, f32 = jnp.bfloat16, jnp.float32
    own, sib = (own0, own1), (sib0, sib1)

    def remote(src, dst, send, recv, band, patch):
        return pltpu.make_async_remote_copy(
            src_ref=src, dst_ref=dst, send_sem=send, recv_sem=recv,
            device_id={"band": band, "patch": patch}, device_id_type=pl.DeviceIdType.MESH,
        )

    home = b // g
    home_here = home // 2 == q
    own_source = b % g

    def source(jj):
        j = (x + jj) % g
        band = p * g + j
        on_line = jj % 2 == 0 if g % 2 == 0 else band % 2 == x
        return j, band // 2, on_line

    barrier = pltpu.get_barrier_semaphore()

    def greet(band, patch):
        pl.semaphore_signal(
            barrier, inc=1, device_id={"band": band, "patch": patch},
            device_id_type=pl.DeviceIdType.MESH,
        )

    greet(b, 2 * q + 1 - c)
    for d in range(1, n_chips):
        greet(b, 2 * ((q + d) % n_chips) + c)
    greet(2 * z + 1 - x, p)
    greet(2 * ((z + 1) % n_z) + x, p)
    for jj in range(g):
        _, zs, on_line = source(jj)
        if on_line is False:
            continue
        for e in range(np_):
            pp = (p + e) % np_
            sends = (pp // 2 == q) | ((z + zs) % 2 == 0)
            if e == 0:
                sends = sends & (zs != z)
            if on_line is not True:
                sends = sends & on_line
            when(sends, lambda zs=zs, pp=pp: greet(2 * zs + x, pp))
    greetings = n_chips + 2 + jnp.where(home_here, n_z - (home == p).astype(jnp.int32), n_z // 2)

    depth = mesh_dev // lat_sem.shape[0]
    lat_copies = [
        pltpu.make_async_copy(
            latents.at[pl.ds(k * depth, depth)], lat.at[pl.ds(k * depth, depth)], lat_sem.at[k]
        )
        for k in range(lat_sem.shape[0])
    ]
    mine_copies = [pltpu.make_async_copy(pieces.at[i], mine.at[i], mine_sem.at[i]) for i in range(tb)]
    for copy in mine_copies + lat_copies:
        copy.start()
    w1_copy = pltpu.make_async_copy(w_first, w1, wt_sem.at[0])
    w2_copy = pltpu.make_async_copy(w_second, w2, wt_sem.at[1])
    w1_copy.start()
    w2_copy.start()

    owner = [owners[t] for t in range(tiles)]
    rank = []
    for t in range(tiles):
        r = jnp.int32(0)
        for u in range(t):
            r = r + (owner[u] == owner[t]).astype(jnp.int32)
        rank.append(r)
        rank_of[t] = jnp.minimum(r, slots - 1)
    mark = [jnp.where(owner[t] == p, rank[t], -1) for t in range(tiles)]
    perm[...] = jnp.full(perm.shape, -1, jnp.int32)
    for s in range(slots):
        tile = jnp.int32(0)
        for t in range(tiles):
            tile = tile + jnp.where(mark[t] == s, t, 0)
        perm[s : s + 1, :] = rows[pl.ds(tile, 1), :]
    columns = perm[...].T
    iota = lax.broadcasted_iota(jnp.int32, (blk, mesh_dev), 1)
    for s in range(slots):
        hit = iota == columns[:, s : s + 1]
        onehot[s * blk : (s + 1) * blk, :] = jnp.where(hit, 1.0, 0.0).astype(bf16)

    pl.semaphore_wait(barrier, greetings)

    def piece_copy(i, dz):
        return remote(
            mine.at[i],
            weights.at[own_source * tb + i, pl.ds(pl.multiple_of(p * cl, cl), cl)],
            piece_send.at[i, dz], w_recv.at[own_source, i, p],
            2 * ((z + dz) % n_z) + x, home,
        )

    def piece_sends(dz):
        if dz == 0:
            return home != p
        return home_here if dz % 2 else True

    away = sorted(range(n_z), key=lambda dz: -min(dz, n_z - dz))
    for i in range(tb):
        mine_copies[i].wait()
        for dz in away:
            when(piece_sends(dz), lambda i=i, dz=dz: piece_copy(i, dz).start())

    @pl.when(home == p)
    def _():
        for i in range(tb):
            pltpu.make_async_copy(
                pieces.at[i],
                weights.at[own_source * tb + i, pl.ds(pl.multiple_of(p * cl, cl), cl)],
                w_recv.at[own_source, i, p],
            ).start()

    def chunk(j, i, at):
        part = weights.at[j * tb + i, pl.ds(pl.multiple_of(at * cl, cl), cl)]
        return part, w_recv.at[j, i, at]

    def arrive(j, i, at):
        part, recv = chunk(j, i, at)
        pltpu.make_async_copy(part, part, recv).wait()

    def along_z(j, i, at):
        part, recv = chunk(j, i, at)
        return remote(part, part, z_send.at[i, at], recv, 2 * ((z + n_z - 1) % n_z) + x, p)

    def along_x(j, i, at):
        part, recv = chunk(j, i, at)
        return remote(part, part, x_send.at[i, at], recv, 2 * z + 1 - x, p)

    def each_chunk(jj, i, dd, act):
        j, zs, on_line = source(jj)

        def body():
            for half in range(2):
                act(j, zs, i, dd, ((q + dd) % n_chips) * 2 + half)

        when(on_line, body)

    def relay_one(j, zs, i, dd, at):
        arrive(j, i, at)
        if dd:
            pl.when((z + zs) % 2 == 0)(lambda: along_z(j, i, at).start())
        along_x(j, i, at).start()

    def drain_one(j, zs, i, dd, at):
        if dd:
            pl.when((z + zs) % 2 == 0)(lambda: along_z(j, i, at).wait_send())
        along_x(j, i, at).wait_send()

    def relay(i, dd):
        for jj in range(g):
            each_chunk(jj, i, dd, relay_one)

    per = slots // PARTS

    def to_sibling(h, k):
        at = pl.ds(k * per, per)
        return remote(
            own[h].at[at], sib[h].at[at], sib_send.at[h, k], sib_recv.at[h, k], b, 2 * q + 1 - c
        )

    for copy in lat_copies:
        copy.wait()
    for h in range(2):
        for k in range(PARTS):
            part = jnp.dot(
                onehot[k * per * blk : (k + 1) * per * blk, :], lat[:, h * wide : (h + 1) * wide],
                preferred_element_type=f32,
            )
            own[h][k * per : (k + 1) * per] = part.astype(bf16).reshape(per, blk, wide)
            to_sibling(h, k).start()

    def tile_of(kk):
        return ((x + kk // tb) % g) * tb + kk % tb

    def from_this_chip(h, t):
        return jnp.where(owners[t] == p, own[h][rank_of[t]], sib[h][rank_of[t]])

    def to_chip(h, d, kk):
        return remote(
            far.at[h, d - 1, kk], from_chip.at[h, d - 1, kk],
            chip_send.at[h, d - 1, kk], chip_recv.at[h, d - 1, kk],
            b, 2 * ((q + d) % n_chips) + c,
        )

    def send_far(h):
        for k in range(PARTS):
            to_sibling(h, k).wait_recv()
        for kk in range(tp):
            for d in range(1, n_chips):
                t = (2 * ((q + d) % n_chips) + c) * tp + tile_of(kk)
                far[h, d - 1, kk] = from_this_chip(h, t)
                to_chip(h, d, kk).start()

    send_far(0)
    relay(0, 0)
    send_far(1)
    for i in range(tb):
        for dd in range(n_chips):
            if i or dd:
                relay(i, dd)

    w1_copy.wait()
    w2_copy.wait()
    eye = jnp.where(
        lax.broadcasted_iota(jnp.int32, (width, width), 0)
        == lax.broadcasted_iota(jnp.int32, (width, width), 1), 1.0, 0.0,
    ).astype(bf16)
    w1t[...] = (0.5 * contract_last(eye, w1[...])).astype(bf16)
    w2e[EXT:, :] = contract_last(eye, w2[...]).astype(bf16)
    pad = EXT // 2
    scaled = jnp.concatenate(
        [w_out[...].astype(f32) * w_gain[...], jnp.zeros((pad - channels, width), f32)], axis=0
    )
    high, rest = split(scaled)
    mid, rest = split(rest)
    ones = jnp.full((pad, width), 1.0 / width, f32).astype(bf16)
    sums = contract_last(jnp.concatenate([high, mid, rest.astype(bf16), ones], axis=0), w2[...])
    mean_row = sums[3 * pad : 3 * pad + 1]
    head = sums[:pad] + sums[pad : 2 * pad] + sums[2 * pad : 3 * pad]
    head = head - jnp.sum(scaled, axis=1, keepdims=True) * mean_row
    head = jnp.where(lax.broadcasted_iota(jnp.int32, head.shape, 0) == channels, mean_row, head)
    high, rest = split(head)
    w2e[:pad, :] = high
    w2e[pad:EXT, :] = rest.astype(bf16)
    b2c = w_b2[...] - jnp.mean(w_b2[...], axis=1, keepdims=True)
    head_bias = jnp.sum(scaled * b2c, axis=1, keepdims=True)
    b2b[...] = jnp.transpose(jnp.broadcast_to(b2c, (128, width)))
    high, rest = split(jnp.transpose(jnp.broadcast_to(0.5 * w_b1[...], (128, width))))
    mid, rest = split(rest)
    lane = lax.broadcasted_iota(jnp.int32, (width, 128), 1)
    terms = (high.astype(f32), mid.astype(f32), rest)
    bias_columns = jnp.zeros((width, 128), f32)
    for k, term in enumerate(terms):
        bias_columns = jnp.where(lane == k, term, bias_columns)
    bft[:, blk:] = bias_columns.astype(bf16)
    diagonal = lax.broadcasted_iota(jnp.int32, (pad, channels), 0) == lax.broadcasted_iota(
        jnp.int32, (pad, channels), 1
    )
    bias = jnp.sum(jnp.where(diagonal, w_bo[...], 0.0), axis=1, keepdims=True)
    ones_columns = jnp.where(
        lax.broadcasted_iota(jnp.int32, (rows_u, 128), 1) < len(terms), 1.0, 0.0
    ).astype(bf16)

    for kk in range(tp):
        jj, i = kk // tb, kk % tb
        j, _, on_line = source(jj)
        tile = tile_of(kk)
        t = p * tp + tile
        halves = []
        for h in range(2):
            value = from_this_chip(h, t)
            for d in range(1, n_chips):
                to_chip(h, d, kk).wait_recv()
                chip = 2 * ((q + n_chips - d) % n_chips)
                there = (owners[t] == chip) | (owners[t] == chip + 1)
                value = jnp.where(there, from_chip[h, d - 1, kk], value)
            halves.append(value)
        block = jnp.concatenate(halves, axis=1)
        bft[:, :blk] = contract_last(w1t[...], block).astype(bf16)

        for dd in range(n_chips):
            qq = (q + dd) % n_chips

            def rest_arrives():
                for half in range(2):
                    arrive(j, i, qq * 2 + half)

            if on_line is not True:
                when(True if on_line is False else jnp.logical_not(on_line), rest_arrives)
            start = pl.multiple_of(qq * rows_u, rows_u)
            cells = jnp.concatenate([weights[tile, pl.ds(start, rows_u), :], ones_columns], axis=1)
            half_v = contract_last(bft[...], cells)
            hidden = (half_v * jnp.tanh(half_v) + half_v).astype(bf16)
            second = jnp.dot(w2e[...], hidden, preferred_element_type=f32)
            heads = second[:pad] + second[pad:EXT]
            mean = heads[channels : channels + 1]
            centred = second[EXT:] + jnp.concatenate([b2b[...]] * (rows_u // 128), axis=1) - mean
            variance = jnp.sum(centred * centred, axis=0, keepdims=True) * (1.0 / width)
            result = (heads + head_bias) * lax.rsqrt(variance + 1e-05) + bias
            at = pl.multiple_of(tile * (np_ * cl) + start, rows_u)
            for ch in range(channels):
                out[ch, :, pl.ds(at, rows_u)] = result[ch : ch + 1]

    for i in range(tb):
        for dz in away:
            when(piece_sends(dz), lambda i=i, dz=dz: piece_copy(i, dz).wait_send())
    for h in range(2):
        for k in range(PARTS):
            to_sibling(h, k).wait_send()
        for d in range(1, n_chips):
            for kk in range(tp):
                to_chip(h, d, kk).wait_send()
    for jj in range(g):
        for i in range(tb):
            for dd in range(n_chips):
                each_chunk(jj, i, dd, drain_one)


def solution(mesh):
    nb, np_ = mesh.shape["band"], mesh.shape["patch"]

    def body(
        latents, owners, block_rows, pieces, w_first, b_first, w_second, b_second, gain, w_out, b_out
    ):
        tiles, blk = block_rows.shape
        cl, channels = pieces.shape[1], w_out.shape[1]
        mesh_dev, width = latents.shape[1:]
        n_chips, tb, tp = np_ // 2, tiles // nb, tiles // np_
        g = tp // tb
        n_z = nb // 2
        slots = tiles // 2
        far = max(n_chips - 1, 1)
        lat_parts = next(k for k in (5, 4, 2, 1) if mesh_dev % (k * 16) == 0)
        vmem = pl.BlockSpec(memory_space=pltpu.VMEM)
        hbm = pl.BlockSpec(memory_space=pl.ANY)
        bf16 = jnp.bfloat16
        dma = pltpu.SemaphoreType.DMA
        result = pl.pallas_call(
            functools.partial(kernel, nb, np_, tiles, blk, cl, slots),
            out_shape=jax.ShapeDtypeStruct((channels, 1, tp * np_ * cl), jnp.float32),
            in_specs=[pl.BlockSpec(memory_space=pltpu.SMEM)] + [vmem] * 6 + [hbm] * 4,
            out_specs=vmem,
            scratch_shapes=[
                pltpu.VMEM((mesh_dev, width), bf16),
                pltpu.VMEM(w_first.shape[1:], bf16),
                pltpu.VMEM(w_second.shape[1:], bf16),
                pltpu.VMEM((tb, cl, blk), bf16),
                pltpu.VMEM((blk, blk), jnp.int32),
                pltpu.VMEM((slots * blk, mesh_dev), bf16),
            ]
            + [pltpu.VMEM((slots, blk, width // 2), bf16)] * 4
            + [
                pltpu.VMEM((2, far, tp, blk, width // 2), bf16),
                pltpu.VMEM((2, far, tp, blk, width // 2), bf16),
                pltpu.VMEM((tp, np_ * cl, blk), bf16),
                pltpu.VMEM((width, width), bf16),
                pltpu.VMEM((EXT + width, width), bf16),
                pltpu.VMEM((width, 128), jnp.float32),
                pltpu.VMEM((width, blk + 128), bf16),
                pltpu.SMEM((tiles,), jnp.int32),
                dma((lat_parts,)),
                dma((2,)),
                dma((tb,)),
                dma((tb, n_z)),
                dma((g, tb, np_)),
                dma((tb, np_)),
                dma((tb, np_)),
                dma((2, PARTS)),
                dma((2, PARTS)),
                dma((2, far, tp)),
                dma((2, far, tp)),
            ],
            compiler_params=pltpu.CompilerParams(collective_id=0, has_side_effects=True),
            name="decode",
        )(
            owners, block_rows, b_first, b_second, gain, w_out[0], b_out,
            latents[0], pieces, w_first[0], w_second[0],
        )
        return jnp.transpose(result, (1, 0, 2))

    return jax.shard_map(
        body,
        mesh=mesh,
        in_specs=(
            P("band", "patch", None),
            P(),
            P(),
            P("band", "patch", None),
            P("band", None, None),
            P("band", None),
            P("band", None, None),
            P("band", None),
            P("band", None),
            P("band", None, None),
            P("band", None),
        ),
        out_specs=P("band", None, "patch"),
        check_vma=False,
    )
```

time: 36.5 us -> 32.8 us (0.90)
  the two profiles are of different devices: /device:TPU:5 before, /device:TPU:17 now
where the time goes in v1:
time: 32.8 us; the launch traced here: 32.6 us
  Pallas kernels  31 us (95%)
  local copies, waits for them, and re-layouts  1.62 us (5%)
    pallas_call x1, Pallas kernels, body(): pl.pallas_call(functools.partial(kernel, nb, np_, tiles, blk, cl, slots),...  31 us
    unnamed x1, local copies, waits for them, and re-layouts  1.62 us

profile of v1, /device:TPU:17, one launch (start us, length us, event | category | flops | bytes accessed | tf_op | source)
XLA Modules:
  0.0 32.6 jit_solution(13812013389568276300)
XLA Ops:
  0.0 31.0 %decode.1 = f32[12,1,4096]{2,1,0:T(1,128)} custom-call(s32[16]{0:T(128)} %owners.1, s32[16,128]{1,0:T(8,128)} %rows.1, f32[1,512]{1,0:T(1,128)} %w_b1.1, f32[1,512]{1,0:T(1,128)} %w_b2.1, f32[1,512]{1,0:T(1,128)} %w_gain.1, bf16[12,512]{1,0:T(8,128)(2,1)} %bitcast.9, f32[1,12]{1,0:T(1,128)} %w_bo.1, bf16[2560,512]{1,0:T(8,128)(2,1)} %bitcast.5, ...), custom_call_target="tpu_custom_call" | custom-call | tf_op jit(solution)/shard_map/decode/pallas_call | solution.py:367
  31.0 1.6 %copy.13 = f32[1,12,4096]{2,0,1:T(1,128)} copy(f32[1,12,4096]{2,0,1:T(1,128)} %bitcast.6) | data formatting | bytes 393216

commit v2 on v1

--- a/solution.py
+++ b/solution.py
@@ -29,12 +29,12 @@
 
 def kernel(
     nb, np_, tiles, blk, cl, slots,
-    owners, rows, w_b1, w_b2, w_gain, w_out, w_bo, latents, pieces, w_first, w_second,
+    owners_in, rows_in, b1_in, b2_in, gain_in, out_in, bo_in, latents, pieces, w_first, w_second,
     out,
-    lat, w1, w2, mine, perm, onehot, own0, own1, sib0, sib1, far, from_chip, weights,
-    w1t, w2e, b2b, bft, rank_of,
-    lat_sem, wt_sem, mine_sem, piece_send, w_recv, z_send, x_send,
-    sib_send, sib_recv, chip_send, chip_recv,
+    owners, rows, w_b1, w_b2, w_gain, w_out, w_bo, lat, w1, w2, mine, perm, onehot, own0, own1, sib0, sib1, far, from_chip, weights,
+    w1t, w2e, b2b, bft, fields, rank_of,
+    small_sem, lat_sem, wt_sem, mine_sem, piece_send, w_recv, z_send, x_send,
+    sib_send, sib_recv, chip_send, chip_recv, out_sem,
 ):
     b, p = lax.axis_index("band"), lax.axis_index("patch")
     n_chips = np_ // 2
@@ -45,7 +45,7 @@
     z, x = b // 2, b % 2
     mesh_dev, width = latents.shape
     wide = width // 2
-    rows_u = 2 * cl
+    in_tile = np_ * cl
     channels = w_bo.shape[1]
     bf16, f32 = jnp.bfloat16, jnp.float32
     own, sib = (own0, own1), (sib0, sib1)
@@ -59,6 +59,12 @@
     home = b // g
     home_here = home // 2 == q
     own_source = b % g
+
+    n_pair = n_z // 2
+    pair = z + 1 - 2 * (z % 2)
+
+    def seed(m):
+        return 2 * ((z // 2 + m) % n_pair) + z % 2
 
     def source(jj):
         j = (x + jj) % g
@@ -66,6 +72,11 @@
         on_line = jj % 2 == 0 if g % 2 == 0 else band % 2 == x
         return j, band // 2, on_line
 
+    def place(zs):
+        return jnp.where(
+            z // 2 == zs // 2, jnp.where(z == zs, 0, 1), jnp.where(z % 2 == zs % 2, 2, 3)
+        )
+
     barrier = pltpu.get_barrier_semaphore()
 
     def greet(band, patch):
@@ -78,20 +89,25 @@
     for d in range(1, n_chips):
         greet(b, 2 * ((q + d) % n_chips) + c)
     greet(2 * z + 1 - x, p)
-    greet(2 * ((z + 1) % n_z) + x, p)
+    greet(2 * pair + x, p)
+    for m in range(1, n_pair):
+        greet(2 * seed(m) + x, p)
     for jj in range(g):
         _, zs, on_line = source(jj)
         if on_line is False:
             continue
+        at_line = place(zs)
         for e in range(np_):
             pp = (p + e) % np_
-            sends = (pp // 2 == q) | ((z + zs) % 2 == 0)
+            across = (at_line == 0) | (at_line == 2) if tb > 1 else at_line == 0
+            sends = jnp.where(pp // 2 == q, at_line != 3, across)
             if e == 0:
-                sends = sends & (zs != z)
+                sends = sends & (at_line != 0)
             if on_line is not True:
                 sends = sends & on_line
             when(sends, lambda zs=zs, pp=pp: greet(2 * zs + x, pp))
-    greetings = n_chips + 2 + jnp.where(home_here, n_z - (home == p).astype(jnp.int32), n_z // 2)
+    outgoing = n_pair + 1 - (home == p).astype(jnp.int32)
+    greetings = n_chips + 1 + n_pair + jnp.where(home_here, outgoing, n_pair if tb > 1 else 1)
 
     depth = mesh_dev // lat_sem.shape[0]
     lat_copies = [
@@ -101,13 +117,22 @@
         for k in range(lat_sem.shape[0])
     ]
     mine_copies = [pltpu.make_async_copy(pieces.at[i], mine.at[i], mine_sem.at[i]) for i in range(tb)]
-    for copy in mine_copies + lat_copies:
+    small = [
+        pltpu.make_async_copy(src, dst, small_sem.at[k])
+        for k, (src, dst) in enumerate((
+            (owners_in, owners), (rows_in, rows), (b1_in, w_b1), (b2_in, w_b2),
+            (gain_in, w_gain), (out_in, w_out), (bo_in, w_bo),
+        ))
+    ]
+    for copy in small[:2] + lat_copies + mine_copies + small[2:]:
         copy.start()
     w1_copy = pltpu.make_async_copy(w_first, w1, wt_sem.at[0])
     w2_copy = pltpu.make_async_copy(w_second, w2, wt_sem.at[1])
     w1_copy.start()
     w2_copy.start()
 
+    for copy in small[:2]:
+        copy.wait()
     owner = [owners[t] for t in range(tiles)]
     rank = []
     for t in range(tiles):
@@ -124,40 +149,37 @@
             tile = tile + jnp.where(mark[t] == s, t, 0)
         perm[s : s + 1, :] = rows[pl.ds(tile, 1), :]
     columns = perm[...].T
-    iota = lax.broadcasted_iota(jnp.int32, (blk, mesh_dev), 1)
-    for s in range(slots):
-        hit = iota == columns[:, s : s + 1]
-        onehot[s * blk : (s + 1) * blk, :] = jnp.where(hit, 1.0, 0.0).astype(bf16)
-
-    pl.semaphore_wait(barrier, greetings)
-
-    def piece_copy(i, dz):
+    def piece_copy(i, k):
         return remote(
             mine.at[i],
             weights.at[own_source * tb + i, pl.ds(pl.multiple_of(p * cl, cl), cl)],
-            piece_send.at[i, dz], w_recv.at[own_source, i, p],
-            2 * ((z + dz) % n_z) + x, home,
-        )
-
-    def piece_sends(dz):
-        if dz == 0:
+            piece_send.at[i, k], w_recv.at[own_source, i, p],
+            2 * (seed(k) if k < n_pair else pair) + x, home,
+        )
+
+    def piece_sends(i, k):
+        if k == 0:
             return home != p
-        return home_here if dz % 2 else True
-
-    away = sorted(range(n_z), key=lambda dz: -min(dz, n_z - dz))
-    for i in range(tb):
-        mine_copies[i].wait()
-        for dz in away:
-            when(piece_sends(dz), lambda i=i, dz=dz: piece_copy(i, dz).start())
-
-    @pl.when(home == p)
-    def _():
+        if k == n_pair or i % 2 == 0:
+            return home_here
+        return True
+
+    away = list(range(1, n_pair + 1)) + [0]
+
+    def send_pieces():
         for i in range(tb):
-            pltpu.make_async_copy(
-                pieces.at[i],
-                weights.at[own_source * tb + i, pl.ds(pl.multiple_of(p * cl, cl), cl)],
-                w_recv.at[own_source, i, p],
-            ).start()
+            mine_copies[i].wait()
+            for k in away:
+                when(piece_sends(i, k), lambda i=i, k=k: piece_copy(i, k).start())
+
+        @pl.when(home == p)
+        def _():
+            for i in range(tb):
+                pltpu.make_async_copy(
+                    pieces.at[i],
+                    weights.at[own_source * tb + i, pl.ds(pl.multiple_of(p * cl, cl), cl)],
+                    w_recv.at[own_source, i, p],
+                ).start()
 
     def chunk(j, i, at):
         part = weights.at[j * tb + i, pl.ds(pl.multiple_of(at * cl, cl), cl)]
@@ -167,37 +189,42 @@
         part, recv = chunk(j, i, at)
         pltpu.make_async_copy(part, part, recv).wait()
 
-    def along_z(j, i, at):
+    def along_z(j, i, at, k):
         part, recv = chunk(j, i, at)
-        return remote(part, part, z_send.at[i, at], recv, 2 * ((z + n_z - 1) % n_z) + x, p)
+        return remote(part, part, z_send.at[k, i, at], recv, 2 * (seed(k) if k else pair) + x, p)
 
     def along_x(j, i, at):
         part, recv = chunk(j, i, at)
         return remote(part, part, x_send.at[i, at], recv, 2 * z + 1 - x, p)
 
-    def each_chunk(jj, i, dd, act):
-        j, zs, on_line = source(jj)
-
-        def body():
-            for half in range(2):
-                act(j, zs, i, dd, ((q + dd) % n_chips) * 2 + half)
-
-        when(on_line, body)
-
-    def relay_one(j, zs, i, dd, at):
-        arrive(j, i, at)
-        if dd:
-            pl.when((z + zs) % 2 == 0)(lambda: along_z(j, i, at).start())
-        along_x(j, i, at).start()
-
-    def drain_one(j, zs, i, dd, at):
-        if dd:
-            pl.when((z + zs) % 2 == 0)(lambda: along_z(j, i, at).wait_send())
-        along_x(j, i, at).wait_send()
-
-    def relay(i, dd):
+    def onward(at_line, j, i, dd, at):
+        copies = []
+        if at_line == 2 or (at_line == 0 and dd):
+            copies.append(along_z(j, i, at, 0))
+        if at_line == 0 and dd and i % 2 == 0:
+            copies += [along_z(j, i, at, m) for m in range(1, n_pair)]
+        return copies + [along_x(j, i, at)]
+
+    def relay(at_line, chunks, act="relay"):
         for jj in range(g):
-            each_chunk(jj, i, dd, relay_one)
+            j, zs, on_line = source(jj)
+            if on_line is False:
+                continue
+
+            def body(j=j):
+                for i, dd in chunks:
+                    for half in range(2):
+                        at = ((q + dd) % n_chips) * 2 + half
+                        if act == "relay":
+                            arrive(j, i, at)
+                        for copy in onward(at_line, j, i, dd, at):
+                            if act == "relay":
+                                copy.start()
+                            else:
+                                copy.wait_send()
+
+            here = place(zs) == at_line
+            when(here if on_line is True else here & on_line, body)
 
     per = slots // PARTS
 
@@ -207,16 +234,41 @@
             own[h].at[at], sib[h].at[at], sib_send.at[h, k], sib_recv.at[h, k], b, 2 * q + 1 - c
         )
 
-    for copy in lat_copies:
-        copy.wait()
-    for h in range(2):
-        for k in range(PARTS):
-            part = jnp.dot(
+    def gather(h):
+        done = [
+            jnp.dot(
                 onehot[k * per * blk : (k + 1) * per * blk, :], lat[:, h * wide : (h + 1) * wide],
                 preferred_element_type=f32,
             )
-            own[h][k * per : (k + 1) * per] = part.astype(bf16).reshape(per, blk, wide)
-            to_sibling(h, k).start()
+            for k in range(PARTS)
+        ]
+        for k in range(PARTS):
+            own[h][k * per : (k + 1) * per] = done[k].astype(bf16).reshape(per, blk, wide)
+
+    def front(send):
+        iota = lax.broadcasted_iota(jnp.int32, (blk, mesh_dev), 1)
+        for s in range(slots):
+            hit = iota == columns[:, s : s + 1]
+            onehot[s * blk : (s + 1) * blk, :] = jnp.where(hit, 1.0, 0.0).astype(bf16)
+        for copy in lat_copies:
+            copy.wait()
+        for h in range(2):
+            gather(h)
+            if send:
+                for k in range(PARTS):
+                    to_sibling(h, k).start()
+
+    pl.when(z == 0)(lambda: front(False))
+    pl.semaphore_wait(barrier, greetings)
+    send_pieces()
+
+    @pl.when(z == 0)
+    def _():
+        for h in range(2):
+            for k in range(PARTS):
+                to_sibling(h, k).start()
+
+    pl.when(z != 0)(lambda: front(True))
 
     def tile_of(kk):
         return ((x + kk // tb) % g) * tb + kk % tb
@@ -231,23 +283,29 @@
             b, 2 * ((q + d) % n_chips) + c,
         )
 
-    def send_far(h):
+    def send_far(h, kk):
+        for d in range(1, n_chips):
+            t = (2 * ((q + d) % n_chips) + c) * tp + tile_of(kk)
+            far[h, d - 1, kk] = from_this_chip(h, t)
+            to_chip(h, d, kk).start()
+
+    def sibling_here(h):
         for k in range(PARTS):
             to_sibling(h, k).wait_recv()
-        for kk in range(tp):
-            for d in range(1, n_chips):
-                t = (2 * ((q + d) % n_chips) + c) * tp + tile_of(kk)
-                far[h, d - 1, kk] = from_this_chip(h, t)
-                to_chip(h, d, kk).start()
-
-    send_far(0)
-    relay(0, 0)
-    send_far(1)
-    for i in range(tb):
-        for dd in range(n_chips):
-            if i or dd:
-                relay(i, dd)
-
+
+    sibling_here(0)
+    first = max(tp // 2, 1)
+    for kk in range(first):
+        send_far(0, kk)
+    every = [(i, 0) for i in range(tb)]
+    across = [(i, dd) for i in range(tb) for dd in range(1, n_chips)]
+    back = [(i, dd) for i in reversed(range(tb)) for dd in range(1, n_chips)]
+    early = {0: every + across[: n_chips - 1], 1: every[:1], 2: every[:1], 3: []}
+    late = {0: across[n_chips - 1 :], 1: every[1:] + across, 2: every[1:] + back, 3: every + back}
+    for k in range(4):
+        relay(k, early[k])
+    for copy in small[2:]:
+        copy.wait()
     w1_copy.wait()
     w2_copy.wait()
     eye = jnp.where(
@@ -287,8 +345,23 @@
     )
     bias = jnp.sum(jnp.where(diagonal, w_bo[...], 0.0), axis=1, keepdims=True)
     ones_columns = jnp.where(
-        lax.broadcasted_iota(jnp.int32, (rows_u, 128), 1) < len(terms), 1.0, 0.0
+        lax.broadcasted_iota(jnp.int32, (in_tile, 128), 1) < len(terms), 1.0, 0.0
     ).astype(bf16)
+
+    sibling_here(1)
+    for kk in range(first):
+        send_far(1, kk)
+    for kk in range(first, tp):
+        for h in range(2):
+            send_far(h, kk)
+    for k in range(4):
+        relay(k, late[k])
+
+    def out_copy(kk, tile):
+        cells = pl.ds(pl.multiple_of(tile * in_tile, in_tile), in_tile)
+        return pltpu.make_async_copy(
+            fields.at[:, :, cells], out.at[:, :, cells], out_sem.at[kk]
+        )
 
     for kk in range(tp):
         jj, i = kk // tb, kk % tb
@@ -305,44 +378,43 @@
                 value = jnp.where(there, from_chip[h, d - 1, kk], value)
             halves.append(value)
         block = jnp.concatenate(halves, axis=1)
-        bft[:, :blk] = contract_last(w1t[...], block).astype(bf16)
-
-        for dd in range(n_chips):
-            qq = (q + dd) % n_chips
-
-            def rest_arrives():
-                for half in range(2):
-                    arrive(j, i, qq * 2 + half)
-
-            if on_line is not True:
-                when(True if on_line is False else jnp.logical_not(on_line), rest_arrives)
-            start = pl.multiple_of(qq * rows_u, rows_u)
-            cells = jnp.concatenate([weights[tile, pl.ds(start, rows_u), :], ones_columns], axis=1)
-            half_v = contract_last(bft[...], cells)
-            hidden = (half_v * jnp.tanh(half_v) + half_v).astype(bf16)
-            second = jnp.dot(w2e[...], hidden, preferred_element_type=f32)
-            heads = second[:pad] + second[pad:EXT]
-            mean = heads[channels : channels + 1]
-            centred = second[EXT:] + jnp.concatenate([b2b[...]] * (rows_u // 128), axis=1) - mean
-            variance = jnp.sum(centred * centred, axis=0, keepdims=True) * (1.0 / width)
-            result = (heads + head_bias) * lax.rsqrt(variance + 1e-05) + bias
-            at = pl.multiple_of(tile * (np_ * cl) + start, rows_u)
-            for ch in range(channels):
-                out[ch, :, pl.ds(at, rows_u)] = result[ch : ch + 1]
+
+        def rest_arrives(j=j, i=i):
+            for at in range(np_):
+                arrive(j, i, at)
+
+        if on_line is not True:
+            when(True if on_line is False else jnp.logical_not(on_line), rest_arrives)
+        for r in range(2):
+            at = slice(r * wide, (r + 1) * wide)
+            bft[at, :blk] = contract_last(w1t[at, :], block).astype(bf16)
+        cells = jnp.concatenate([weights[tile], ones_columns], axis=1)
+        half_v = contract_last(bft[...], cells)
+        hidden = (half_v * jnp.tanh(half_v) + half_v).astype(bf16)
+        second = jnp.dot(w2e[...], hidden, preferred_element_type=f32)
+        heads = second[:pad] + second[pad:EXT]
+        mean = heads[channels : channels + 1]
+        centred = second[EXT:] + jnp.concatenate([b2b[...]] * (in_tile // 128), axis=1) - mean
+        variance = jnp.sum(centred * centred, axis=0, keepdims=True) * (1.0 / width)
+        result = (heads + head_bias) * lax.rsqrt(variance + 1e-05) + bias
+        at = pl.multiple_of(tile * in_tile, in_tile)
+        for ch in range(channels):
+            fields[ch, :, pl.ds(at, in_tile)] = result[ch : ch + 1]
+        out_copy(kk, tile).start()
 
     for i in range(tb):
-        for dz in away:
-            when(piece_sends(dz), lambda i=i, dz=dz: piece_copy(i, dz).wait_send())
+        for k in away:
+            when(piece_sends(i, k), lambda i=i, k=k: piece_copy(i, k).wait_send())
     for h in range(2):
         for k in range(PARTS):
             to_sibling(h, k).wait_send()
         for d in range(1, n_chips):
             for kk in range(tp):
                 to_chip(h, d, kk).wait_send()
-    for jj in range(g):
-        for i in range(tb):
-            for dd in range(n_chips):
-                each_chunk(jj, i, dd, drain_one)
+    for k in range(4):
+        relay(k, every + across, "drain")
+    for kk in range(tp):
+        out_copy(kk, tile_of(kk)).wait()
 
 
 def solution(mesh):
@@ -360,16 +432,22 @@
         slots = tiles // 2
         far = max(n_chips - 1, 1)
         lat_parts = next(k for k in (5, 4, 2, 1) if mesh_dev % (k * 16) == 0)
-        vmem = pl.BlockSpec(memory_space=pltpu.VMEM)
-        hbm = pl.BlockSpec(memory_space=pl.ANY)
+        hbm = pl.BlockSpec(memory_space=pltpu.HBM)
         bf16 = jnp.bfloat16
         dma = pltpu.SemaphoreType.DMA
         result = pl.pallas_call(
             functools.partial(kernel, nb, np_, tiles, blk, cl, slots),
             out_shape=jax.ShapeDtypeStruct((channels, 1, tp * np_ * cl), jnp.float32),
-            in_specs=[pl.BlockSpec(memory_space=pltpu.SMEM)] + [vmem] * 6 + [hbm] * 4,
-            out_specs=vmem,
+            in_specs=[hbm] * 11,
+            out_specs=hbm,
             scratch_shapes=[
+                pltpu.SMEM((tiles,), jnp.int32),
+                pltpu.VMEM((tiles, blk), jnp.int32),
+                pltpu.VMEM((1, width), jnp.float32),
+                pltpu.VMEM((1, width), jnp.float32),
+                pltpu.VMEM((1, width), jnp.float32),
+                pltpu.VMEM((channels, width), bf16),
+                pltpu.VMEM((1, channels), jnp.float32),
                 pltpu.VMEM((mesh_dev, width), bf16),
                 pltpu.VMEM(w_first.shape[1:], bf16),
                 pltpu.VMEM(w_second.shape[1:], bf16),
@@ -386,18 +464,21 @@
                 pltpu.VMEM((EXT + width, width), bf16),
                 pltpu.VMEM((width, 128), jnp.float32),
                 pltpu.VMEM((width, blk + 128), bf16),
+                pltpu.VMEM((channels, 1, tp * np_ * cl), jnp.float32),
                 pltpu.SMEM((tiles,), jnp.int32),
+                dma((7,)),
                 dma((lat_parts,)),
                 dma((2,)),
                 dma((tb,)),
-                dma((tb, n_z)),
+                dma((tb, n_z // 2 + 1)),
                 dma((g, tb, np_)),
-                dma((tb, np_)),
+                dma((n_z // 2, tb, np_)),
                 dma((tb, np_)),
                 dma((2, PARTS)),
                 dma((2, PARTS)),
                 dma((2, far, tp)),
                 dma((2, far, tp)),
+                dma((tp,)),
             ],
             compiler_params=pltpu.CompilerParams(collective_id=0, has_side_effects=True),
             name="decode",

time: 32.8 us -> 29.4 us (0.90)
  the two profiles are of different devices: /device:TPU:17 before, /device:TPU:5 now
where the time goes in v2:
time: 29.4 us; the launch traced here: 29.3 us
  Pallas kernels  27.6 us (94%)
  local copies, waits for them, and re-layouts  1.62 us (6%)
    pallas_call x1, Pallas kernels, body(): pl.pallas_call(functools.partial(kernel, nb, np_, tiles, blk, cl, slots),...  27.6 us
    unnamed x1, local copies, waits for them, and re-layouts  1.62 us

profile of v2, /device:TPU:5, one launch (start us, length us, event | category | flops | bytes accessed | tf_op | source)
XLA Modules:
  0.0 29.3 jit_solution(14944159300672227048)
XLA Ops:
  0.0 27.6 %decode.1 = f32[12,1,4096]{2,1,0:T(1,128)} custom-call(s32[16]{0:T(128)} %owners_in.1, s32[16,128]{1,0:T(8,128)} %rows_in.1, f32[1,512]{1,0:T(1,128)} %b1_in.1, f32[1,512]{1,0:T(1,128)} %b2_in.1, f32[1,512]{1,0:T(1,128)} %gain_in.1, bf16[12,512]{1,0:T(8,128)(2,1)} %bitcast.9, f32[1,12]{1,0:T(1,128)} %bo_in.1, bf16[2560,512]{1,0:T(8,128)(2,1)} %bitcast.5, ...), custom_call_target="tpu_custom_call" | custom-call | tf_op jit(solution)/shard_map/decode/pallas_call | solution.py:438
  27.7 1.6 %copy.13 = f32[1,12,4096]{2,0,1:T(1,128)} copy(f32[1,12,4096]{2,0,1:T(1,128)} %bitcast.6) | data formatting | bytes 393216

commit v3 on v2

--- a/solution.py
+++ b/solution.py
@@ -31,7 +31,7 @@
     nb, np_, tiles, blk, cl, slots,
     owners_in, rows_in, b1_in, b2_in, gain_in, out_in, bo_in, latents, pieces, w_first, w_second,
     out,
-    owners, rows, w_b1, w_b2, w_gain, w_out, w_bo, lat, w1, w2, mine, perm, onehot, own0, own1, sib0, sib1, far, from_chip, weights,
+    owners, rows, w_rows, w_out, w_bo, lat, w_both, mine, perm, onehot, own0, own1, sib0, sib1, far, from_chip, weights,
     w1t, w2e, b2b, bft, fields, rank_of,
     small_sem, lat_sem, wt_sem, mine_sem, piece_send, w_recv, z_send, x_send,
     sib_send, sib_recv, chip_send, chip_recv, out_sem,
@@ -94,42 +94,41 @@
         greet(2 * seed(m) + x, p)
     for jj in range(g):
         _, zs, on_line = source(jj)
-        if on_line is False:
-            continue
         at_line = place(zs)
         for e in range(np_):
             pp = (p + e) % np_
-            across = (at_line == 0) | (at_line == 2) if tb > 1 else at_line == 0
-            sends = jnp.where(pp // 2 == q, at_line != 3, across)
-            if e == 0:
-                sends = sends & (at_line != 0)
+            if on_line is not False:
+                sends = (at_line % 2 == 0) | ((pp // 2 == q) & (at_line == 1))
+                if e == 0:
+                    sends = sends & (at_line != 0)
+                if on_line is not True:
+                    sends = sends & on_line
+                when(sends, lambda zs=zs, pp=pp: greet(2 * zs + x, pp))
             if on_line is not True:
-                sends = sends & on_line
-            when(sends, lambda zs=zs, pp=pp: greet(2 * zs + x, pp))
-    outgoing = n_pair + 1 - (home == p).astype(jnp.int32)
-    greetings = n_chips + 1 + n_pair + jnp.where(home_here, outgoing, n_pair if tb > 1 else 1)
-
-    depth = mesh_dev // lat_sem.shape[0]
-    lat_copies = [
-        pltpu.make_async_copy(
-            latents.at[pl.ds(k * depth, depth)], lat.at[pl.ds(k * depth, depth)], lat_sem.at[k]
-        )
-        for k in range(lat_sem.shape[0])
-    ]
-    mine_copies = [pltpu.make_async_copy(pieces.at[i], mine.at[i], mine_sem.at[i]) for i in range(tb)]
+                sends = (pp // 2 == q) & (at_line == 0)
+                if on_line is not False:
+                    sends = sends & jnp.logical_not(on_line)
+                when(sends, lambda zs=zs, pp=pp: greet(2 * zs + 1 - x, pp))
+    outgoing = n_pair + 2 - (home == p).astype(jnp.int32)
+    greetings = n_chips + 1 + n_pair + jnp.where(home_here, outgoing, n_pair)
+
+    lat_copy = pltpu.make_async_copy(latents, lat, lat_sem.at[0])
+    mine_copy = pltpu.make_async_copy(pieces, mine, mine_sem.at[0])
     small = [
         pltpu.make_async_copy(src, dst, small_sem.at[k])
         for k, (src, dst) in enumerate((
-            (owners_in, owners), (rows_in, rows), (b1_in, w_b1), (b2_in, w_b2),
-            (gain_in, w_gain), (out_in, w_out), (bo_in, w_bo),
+            (owners_in, owners), (rows_in, rows), (out_in, w_out), (bo_in, w_bo),
         ))
     ]
-    for copy in small[:2] + lat_copies + mine_copies + small[2:]:
+    rows_of_width = [
+        pltpu.make_async_copy(src, w_rows.at[k], small_sem.at[4])
+        for k, src in enumerate((b1_in, b2_in, gain_in))
+    ]
+    wide_copies = [
+        pltpu.make_async_copy(src, w_both.at[k], wt_sem.at[0]) for k, src in enumerate((w_first, w_second))
+    ]
+    for copy in small[:2] + [lat_copy, mine_copy] + small[2:] + rows_of_width + wide_copies:
         copy.start()
-    w1_copy = pltpu.make_async_copy(w_first, w1, wt_sem.at[0])
-    w2_copy = pltpu.make_async_copy(w_second, w2, wt_sem.at[1])
-    w1_copy.start()
-    w2_copy.start()
 
     for copy in small[:2]:
         copy.wait()
@@ -153,24 +152,22 @@
         return remote(
             mine.at[i],
             weights.at[own_source * tb + i, pl.ds(pl.multiple_of(p * cl, cl), cl)],
-            piece_send.at[i, k], w_recv.at[own_source, i, p],
-            2 * (seed(k) if k < n_pair else pair) + x, home,
-        )
-
-    def piece_sends(i, k):
+            piece_send.at[k], w_recv.at[own_source, i, p],
+            2 * z + 1 - x if k > n_pair else 2 * (seed(k) if k < n_pair else pair) + x, home,
+        )
+
+    def piece_sends(k):
         if k == 0:
             return home != p
-        if k == n_pair or i % 2 == 0:
-            return home_here
-        return True
-
-    away = list(range(1, n_pair + 1)) + [0]
+        return home_here if k >= n_pair else True
+
+    away = list(range(1, n_pair)) + [n_pair + 1, 0, n_pair]
 
     def send_pieces():
-        for i in range(tb):
-            mine_copies[i].wait()
-            for k in away:
-                when(piece_sends(i, k), lambda i=i, k=k: piece_copy(i, k).start())
+        mine_copy.wait()
+        for k in away:
+            for i in range(tb) if k == 0 else reversed(range(tb)):
+                when(piece_sends(k), lambda i=i, k=k: piece_copy(i, k).start())
 
         @pl.when(home == p)
         def _():
@@ -189,50 +186,89 @@
         part, recv = chunk(j, i, at)
         pltpu.make_async_copy(part, part, recv).wait()
 
-    def along_z(j, i, at, k):
+    def along_z(j, i, at, k, other=0):
         part, recv = chunk(j, i, at)
-        return remote(part, part, z_send.at[k, i, at], recv, 2 * (seed(k) if k else pair) + x, p)
+        return remote(
+            part, part, z_send.at[(k or n_pair) if other else 0], recv, 2 * (seed(k) if k else pair) + x, p
+        )
 
     def along_x(j, i, at):
         part, recv = chunk(j, i, at)
-        return remote(part, part, x_send.at[i, at], recv, 2 * z + 1 - x, p)
+        return remote(part, part, x_send.at[0], recv, 2 * z + 1 - x, p)
+
+    def crosses_early(i, dd):
+        return dd > 0 and i % 2 == 0
 
     def onward(at_line, j, i, dd, at):
         copies = []
         if at_line == 2 or (at_line == 0 and dd):
             copies.append(along_z(j, i, at, 0))
-        if at_line == 0 and dd and i % 2 == 0:
-            copies += [along_z(j, i, at, m) for m in range(1, n_pair)]
-        return copies + [along_x(j, i, at)]
-
-    def relay(at_line, chunks, act="relay"):
+        if (at_line == 0 and dd) or at_line == 1 or (at_line > 1 and not crosses_early(i, dd)):
+            copies.append(along_x(j, i, at))
+        return copies
+
+    def onward_other(at_line, j, i, at):
+        if at_line == 0:
+            return [along_z(j, i, at, m, 1) for m in range(1, n_pair)]
+        return [along_z(j, i, at, 0, 1)]
+
+    def relay(at_line, chunks, other=False):
         for jj in range(g):
             j, zs, on_line = source(jj)
-            if on_line is False:
+            if on_line is other:
                 continue
 
             def body(j=j):
                 for i, dd in chunks:
                     for half in range(2):
                         at = ((q + dd) % n_chips) * 2 + half
-                        if act == "relay":
-                            arrive(j, i, at)
-                        for copy in onward(at_line, j, i, dd, at):
-                            if act == "relay":
-                                copy.start()
-                            else:
-                                copy.wait_send()
+                        arrive(j, i, at)
+                        if other:
+                            copies = onward_other(at_line, j, i, at)
+                        else:
+                            copies = onward(at_line, j, i, dd, at)
+                        for copy in copies:
+                            copy.start()
 
             here = place(zs) == at_line
-            when(here if on_line is True else here & on_line, body)
+            if on_line is not True and on_line is not False:
+                here = here & (jnp.logical_not(on_line) if other else on_line)
+            if chunks:
+                when(here, body)
+
+    def sent(sem, count):
+        if count:
+            a = next(a for a in range(1, tp + 1) if count % a == 0 and count // a <= np_)
+            part = weights.at[pl.ds(0, a), pl.ds(0, count // a * cl)]
+            remote(part, part, sem, w_recv.at[0, 0, 0], 2 * z + 1 - x, p).wait_send()
+
+    def relay_drain(at_line):
+        across = [(i, dd) for i in range(tb) for dd in range(1, n_chips)]
+        even = [1 for i, dd in across if crosses_early(i, dd)]
+        in_plane, over, early = 2 * tb, 2 * len(across), 2 * len(even)
+        along = {0: over, 1: 0, 2: in_plane + over, 3: 0}[at_line]
+        beside = {0: over, 1: in_plane + over, 2: in_plane + over - early, 3: in_plane + over - early}[at_line]
+        for jj in range(g):
+            _, zs, on_line = source(jj)
+            here = place(zs) == at_line
+
+            def body():
+                sent(z_send.at[0], along)
+                sent(x_send.at[0], beside)
+
+            def body_other():
+                for m in range(1, n_pair) if at_line == 0 else (n_pair,):
+                    sent(z_send.at[m], early)
+
+            if on_line is not False:
+                when(here if on_line is True else here & on_line, body)
+            if on_line is not True and at_line % 2 == 0:
+                when(here if on_line is False else here & jnp.logical_not(on_line), body_other)
 
     per = slots // PARTS
 
-    def to_sibling(h, k):
-        at = pl.ds(k * per, per)
-        return remote(
-            own[h].at[at], sib[h].at[at], sib_send.at[h, k], sib_recv.at[h, k], b, 2 * q + 1 - c
-        )
+    def to_sibling(h):
+        return remote(own[h], sib[h], sib_send.at[h], sib_recv.at[h], b, 2 * q + 1 - c)
 
     def gather(h):
         done = [
@@ -245,69 +281,86 @@
         for k in range(PARTS):
             own[h][k * per : (k + 1) * per] = done[k].astype(bf16).reshape(per, blk, wide)
 
-    def front(send):
+    def share(h):
+        to_sibling(h).start()
+
+    def front(h):
+        if h == 0:
+            lat_copy.wait()
+        gather(h)
+
+    def build():
         iota = lax.broadcasted_iota(jnp.int32, (blk, mesh_dev), 1)
         for s in range(slots):
             hit = iota == columns[:, s : s + 1]
             onehot[s * blk : (s + 1) * blk, :] = jnp.where(hit, 1.0, 0.0).astype(bf16)
-        for copy in lat_copies:
-            copy.wait()
-        for h in range(2):
-            gather(h)
-            if send:
-                for k in range(PARTS):
-                    to_sibling(h, k).start()
-
-    pl.when(z == 0)(lambda: front(False))
+
+    pl.when(z < n_pair)(build)
+    pl.when(z == 0)(lambda: front(0))
     pl.semaphore_wait(barrier, greetings)
+    pl.when(z == 0)(lambda: share(0))
     send_pieces()
-
-    @pl.when(z == 0)
+    pl.when(z >= n_pair)(build)
+
+    @pl.when(z != 0)
     def _():
-        for h in range(2):
-            for k in range(PARTS):
-                to_sibling(h, k).start()
-
-    pl.when(z != 0)(lambda: front(True))
+        front(0)
+        share(0)
+
+    front(1)
+    share(1)
+
+    def step_of(kk):
+        return kk // tb, tb - 1 - kk % tb
 
     def tile_of(kk):
-        return ((x + kk // tb) % g) * tb + kk % tb
+        jj, i = step_of(kk)
+        return ((x + jj) % g) * tb + i
 
     def from_this_chip(h, t):
         return jnp.where(owners[t] == p, own[h][rank_of[t]], sib[h][rank_of[t]])
 
     def to_chip(h, d, kk):
         return remote(
-            far.at[h, d - 1, kk], from_chip.at[h, d - 1, kk],
-            chip_send.at[h, d - 1, kk], chip_recv.at[h, d - 1, kk],
+            far.at[d - 1, kk, h], from_chip.at[d - 1, kk, h], chip_send.at[0], chip_recv.at[d - 1, kk],
             b, 2 * ((q + d) % n_chips) + c,
         )
+
+    def chip_here(d, kk):
+        part = from_chip.at[d - 1, kk]
+        pltpu.make_async_copy(part, part, chip_recv.at[d - 1, kk]).wait()
 
     def send_far(h, kk):
         for d in range(1, n_chips):
             t = (2 * ((q + d) % n_chips) + c) * tp + tile_of(kk)
-            far[h, d - 1, kk] = from_this_chip(h, t)
+            far[d - 1, kk, h] = from_this_chip(h, t)
             to_chip(h, d, kk).start()
 
     def sibling_here(h):
-        for k in range(PARTS):
-            to_sibling(h, k).wait_recv()
+        to_sibling(h).wait_recv()
 
     sibling_here(0)
     first = max(tp // 2, 1)
     for kk in range(first):
         send_far(0, kk)
-    every = [(i, 0) for i in range(tb)]
-    across = [(i, dd) for i in range(tb) for dd in range(1, n_chips)]
-    back = [(i, dd) for i in reversed(range(tb)) for dd in range(1, n_chips)]
-    early = {0: every + across[: n_chips - 1], 1: every[:1], 2: every[:1], 3: []}
-    late = {0: across[n_chips - 1 :], 1: every[1:] + across, 2: every[1:] + back, 3: every + back}
-    for k in range(4):
-        relay(k, early[k])
+    every = [(i, 0) for i in reversed(range(tb))]
+    even = [(i, dd) for i in range(0, tb, 2) for dd in range(1, n_chips)]
+    odd = [(i, dd) for i in range(1, tb, 2) for dd in range(1, n_chips)]
+    early = {0: even, 2: every[:1]}
+    late = {0: odd + every, 1: every[:1] + odd + every[1:], 2: odd + every[1:] + even, 3: every[:1] + odd}
+    last = {1: even, 3: every[1:] + even}
+
+    @pl.when(z != 0)
+    def _():
+        for k in early:
+            relay(k, early[k])
+
     for copy in small[2:]:
         copy.wait()
-    w1_copy.wait()
-    w2_copy.wait()
+    pltpu.make_async_copy(w_rows, w_rows, small_sem.at[4]).wait()
+    pltpu.make_async_copy(w_both, w_both, wt_sem.at[0]).wait()
+    w1, w2 = w_both.at[0], w_both.at[1]
+    w_b1, w_b2, w_gain = (w_rows.at[k] for k in range(3))
     eye = jnp.where(
         lax.broadcasted_iota(jnp.int32, (width, width), 0)
         == lax.broadcasted_iota(jnp.int32, (width, width), 1), 1.0, 0.0,
@@ -354,34 +407,51 @@
     for kk in range(first, tp):
         for h in range(2):
             send_far(h, kk)
-    for k in range(4):
+    @pl.when(z == 0)
+    def _():
+        for k in early:
+            relay(k, early[k])
+
+    for k in late:
         relay(k, late[k])
+    pl.when(z != 0)(lambda: relay(0, even, other=True))
 
     def out_copy(kk, tile):
         cells = pl.ds(pl.multiple_of(tile * in_tile, in_tile), in_tile)
         return pltpu.make_async_copy(
-            fields.at[:, :, cells], out.at[:, :, cells], out_sem.at[kk]
+            fields.at[:, :, cells], out.at[:, :, cells], out_sem.at[0]
         )
 
     for kk in range(tp):
-        jj, i = kk // tb, kk % tb
-        j, _, on_line = source(jj)
+        jj, i = step_of(kk)
+        j, zs, on_line = source(jj)
+        if kk == min(1, tb - 1):
+            for k in last:
+                relay(k, last[k])
+            pl.when(z == 0)(lambda: relay(0, even, other=True))
+            relay(2, even, other=True)
         tile = tile_of(kk)
         t = p * tp + tile
+        for d in range(1, n_chips):
+            chip_here(d, kk)
         halves = []
         for h in range(2):
             value = from_this_chip(h, t)
             for d in range(1, n_chips):
-                to_chip(h, d, kk).wait_recv()
                 chip = 2 * ((q + n_chips - d) % n_chips)
                 there = (owners[t] == chip) | (owners[t] == chip + 1)
-                value = jnp.where(there, from_chip[h, d - 1, kk], value)
+                value = jnp.where(there, from_chip[d - 1, kk, h], value)
             halves.append(value)
         block = jnp.concatenate(halves, axis=1)
 
-        def rest_arrives(j=j, i=i):
-            for at in range(np_):
-                arrive(j, i, at)
+        def rest_arrives(j=j, i=i, zs=zs):
+            for dd in range(n_chips):
+
+                def wait(dd=dd):
+                    for half in range(2):
+                        arrive(j, i, ((q + dd) % n_chips) * 2 + half)
+
+                when(place(zs) % 2 == 1 if crosses_early(i, dd) else True, wait)
 
         if on_line is not True:
             when(True if on_line is False else jnp.logical_not(on_line), rest_arrives)
@@ -402,19 +472,18 @@
             fields[ch, :, pl.ds(at, in_tile)] = result[ch : ch + 1]
         out_copy(kk, tile).start()
 
-    for i in range(tb):
-        for k in away:
-            when(piece_sends(i, k), lambda i=i, k=k: piece_copy(i, k).wait_send())
+    def pieces_sent(k):
+        return remote(mine, mine, piece_send.at[k], w_recv.at[0, 0, 0], 2 * z + 1 - x, home)
+
+    for k in away:
+        when(piece_sends(k), lambda k=k: pieces_sent(k).wait_send())
     for h in range(2):
-        for k in range(PARTS):
-            to_sibling(h, k).wait_send()
-        for d in range(1, n_chips):
-            for kk in range(tp):
-                to_chip(h, d, kk).wait_send()
+        to_sibling(h).wait_send()
+    if n_chips > 1:
+        remote(far, far, chip_send.at[0], chip_recv.at[0, 0], b, 2 * q + 1 - c).wait_send()
     for k in range(4):
-        relay(k, every + across, "drain")
-    for kk in range(tp):
-        out_copy(kk, tile_of(kk)).wait()
+        relay_drain(k)
+    pltpu.make_async_copy(fields, out, out_sem.at[0]).wait()
 
 
 def solution(mesh):
@@ -431,7 +500,6 @@
         n_z = nb // 2
         slots = tiles // 2
         far = max(n_chips - 1, 1)
-        lat_parts = next(k for k in (5, 4, 2, 1) if mesh_dev % (k * 16) == 0)
         hbm = pl.BlockSpec(memory_space=pltpu.HBM)
         bf16 = jnp.bfloat16
         dma = pltpu.SemaphoreType.DMA
@@ -443,22 +511,19 @@
             scratch_shapes=[
                 pltpu.SMEM((tiles,), jnp.int32),
                 pltpu.VMEM((tiles, blk), jnp.int32),
-                pltpu.VMEM((1, width), jnp.float32),
-                pltpu.VMEM((1, width), jnp.float32),
-                pltpu.VMEM((1, width), jnp.float32),
+                pltpu.VMEM((3, 1, width), jnp.float32),
                 pltpu.VMEM((channels, width), bf16),
                 pltpu.VMEM((1, channels), jnp.float32),
                 pltpu.VMEM((mesh_dev, width), bf16),
-                pltpu.VMEM(w_first.shape[1:], bf16),
-                pltpu.VMEM(w_second.shape[1:], bf16),
+                pltpu.VMEM((2,) + w_first.shape[1:], bf16),
                 pltpu.VMEM((tb, cl, blk), bf16),
                 pltpu.VMEM((blk, blk), jnp.int32),
                 pltpu.VMEM((slots * blk, mesh_dev), bf16),
             ]
             + [pltpu.VMEM((slots, blk, width // 2), bf16)] * 4
             + [
-                pltpu.VMEM((2, far, tp, blk, width // 2), bf16),
-                pltpu.VMEM((2, far, tp, blk, width // 2), bf16),
+                pltpu.VMEM((far, tp, 2, blk, width // 2), bf16),
+                pltpu.VMEM((far, tp, 2, blk, width // 2), bf16),
                 pltpu.VMEM((tp, np_ * cl, blk), bf16),
                 pltpu.VMEM((width, width), bf16),
                 pltpu.VMEM((EXT + width, width), bf16),
@@ -466,19 +531,19 @@
                 pltpu.VMEM((width, blk + 128), bf16),
                 pltpu.VMEM((channels, 1, tp * np_ * cl), jnp.float32),
                 pltpu.SMEM((tiles,), jnp.int32),
-                dma((7,)),
-                dma((lat_parts,)),
+                dma((5,)),
+                dma((1,)),
+                dma((1,)),
+                dma((1,)),
+                dma((n_z // 2 + 2,)),
+                dma((g, tb, np_)),
+                dma((n_z // 2 + 1,)),
+                dma((1,)),
                 dma((2,)),
-                dma((tb,)),
-                dma((tb, n_z // 2 + 1)),
-                dma((g, tb, np_)),
-                dma((n_z // 2, tb, np_)),
-                dma((tb, np_)),
-                dma((2, PARTS)),
-                dma((2, PARTS)),
-                dma((2, far, tp)),
-                dma((2, far, tp)),
-                dma((tp,)),
+                dma((2,)),
+                dma((1,)),
+                dma((far, tp)),
+                dma((1,)),
             ],
             compiler_params=pltpu.CompilerParams(collective_id=0, has_side_effects=True),
             name="decode",

time: 29.4 us -> 25.7 us (0.87)
  Pallas kernels: 27.6 us -> 24 us
    pallas_call x1, Pallas kernels: 27.6 us -> 24 us  [body(): pl.pallas_call(functools.partial(kernel, nb, np_, tiles, blk, cl, slots),...]
where the time goes in v3:
time: 25.7 us; the launch traced here: 25.6 us
  Pallas kernels  24 us (93%)
  local copies, waits for them, and re-layouts  1.62 us (6%)
    pallas_call x1, Pallas kernels, body(): pl.pallas_call(functools.partial(kernel, nb, np_, tiles, blk, cl, slots),...  24 us
    unnamed x1, local copies, waits for them, and re-layouts  1.62 us

profile of v3, /device:TPU:5, one launch (start us, length us, event | category | flops | bytes accessed | tf_op | source)
XLA Modules:
  0.0 25.6 jit_solution(7953400749769406180)
XLA Ops:
  0.0 24.0 %decode.1 = f32[12,1,4096]{2,1,0:T(1,128)} custom-call(s32[16]{0:T(128)} %owners_in.1, s32[16,128]{1,0:T(8,128)} %rows_in.1, f32[1,512]{1,0:T(1,128)} %b1_in.1, f32[1,512]{1,0:T(1,128)} %b2_in.1, f32[1,512]{1,0:T(1,128)} %gain_in.1, bf16[12,512]{1,0:T(8,128)(2,1)} %bitcast.9, f32[1,12]{1,0:T(1,128)} %bo_in.1, bf16[2560,512]{1,0:T(8,128)(2,1)} %bitcast.5, ...), custom_call_target="tpu_custom_call" | custom-call | tf_op jit(solution)/shard_map/decode/pallas_call | solution.py:506
  24.0 1.6 %copy.13 = f32[1,12,4096]{2,0,1:T(1,128)} copy(f32[1,12,4096]{2,0,1:T(1,128)} %bitcast.6) | data formatting | bytes 393216

commit v4 on v3

--- a/solution.py
+++ b/solution.py
@@ -32,9 +32,9 @@
     owners_in, rows_in, b1_in, b2_in, gain_in, out_in, bo_in, latents, pieces, w_first, w_second,
     out,
     owners, rows, w_rows, w_out, w_bo, lat, w_both, mine, perm, onehot, own0, own1, sib0, sib1, far, from_chip, weights,
-    w1t, w2e, b2b, bft, fields, rank_of,
+    w1t, w2e, b2b, bft, rank_of,
     small_sem, lat_sem, wt_sem, mine_sem, piece_send, w_recv, z_send, x_send,
-    sib_send, sib_recv, chip_send, chip_recv, out_sem,
+    sib_send, sib_recv, chip_send, chip_recv,
 ):
     b, p = lax.axis_index("band"), lax.axis_index("patch")
     n_chips = np_ // 2
@@ -416,12 +416,6 @@
         relay(k, late[k])
     pl.when(z != 0)(lambda: relay(0, even, other=True))
 
-    def out_copy(kk, tile):
-        cells = pl.ds(pl.multiple_of(tile * in_tile, in_tile), in_tile)
-        return pltpu.make_async_copy(
-            fields.at[:, :, cells], out.at[:, :, cells], out_sem.at[0]
-        )
-
     for kk in range(tp):
         jj, i = step_of(kk)
         j, zs, on_line = source(jj)
@@ -469,8 +463,7 @@
         result = (heads + head_bias) * lax.rsqrt(variance + 1e-05) + bias
         at = pl.multiple_of(tile * in_tile, in_tile)
         for ch in range(channels):
-            fields[ch, :, pl.ds(at, in_tile)] = result[ch : ch + 1]
-        out_copy(kk, tile).start()
+            out[ch, :, pl.ds(at, in_tile)] = result[ch : ch + 1]
 
     def pieces_sent(k):
         return remote(mine, mine, piece_send.at[k], w_recv.at[0, 0, 0], 2 * z + 1 - x, home)
@@ -483,7 +476,6 @@
         remote(far, far, chip_send.at[0], chip_recv.at[0, 0], b, 2 * q + 1 - c).wait_send()
     for k in range(4):
         relay_drain(k)
-    pltpu.make_async_copy(fields, out, out_sem.at[0]).wait()
 
 
 def solution(mesh):
@@ -505,9 +497,9 @@
         dma = pltpu.SemaphoreType.DMA
         result = pl.pallas_call(
             functools.partial(kernel, nb, np_, tiles, blk, cl, slots),
-            out_shape=jax.ShapeDtypeStruct((channels, 1, tp * np_ * cl), jnp.float32),
+            out_shape=pltpu.VMEM((channels, 1, tp * np_ * cl), jnp.float32),
             in_specs=[hbm] * 11,
-            out_specs=hbm,
+            out_specs=pl.BlockSpec(memory_space=pltpu.VMEM),
             scratch_shapes=[
                 pltpu.SMEM((tiles,), jnp.int32),
                 pltpu.VMEM((tiles, blk), jnp.int32),
@@ -529,7 +521,6 @@
                 pltpu.VMEM((EXT + width, width), bf16),
                 pltpu.VMEM((width, 128), jnp.float32),
                 pltpu.VMEM((width, blk + 128), bf16),
-                pltpu.VMEM((channels, 1, tp * np_ * cl), jnp.float32),
                 pltpu.SMEM((tiles,), jnp.int32),
                 dma((5,)),
                 dma((1,)),
@@ -543,7 +534,6 @@
                 dma((2,)),
                 dma((1,)),
                 dma((far, tp)),
-                dma((1,)),
             ],
             compiler_params=pltpu.CompilerParams(collective_id=0, has_side_effects=True),
             name="decode",

time: 25.7 us -> 24.2 us (0.942)
  local copies, waits for them, and re-layouts: 1.62 us -> 0.68 us
  Pallas kernels: 24 us -> 23.3 us
    unnamed x1, local copies, waits for them, and re-layouts: 1.62 us -> 0.68 us
    pallas_call x1, Pallas kernels: 24 us -> 23.3 us  [body(): pl.pallas_call(functools.partial(kernel, nb, np_, tiles, blk, cl, slots),...]
where the time goes in v4:
time: 24.2 us; the launch traced here: 24 us
  Pallas kernels  23.3 us (96%)
  local copies, waits for them, and re-layouts  0.68 us (3%)
    pallas_call x1, Pallas kernels, body(): pl.pallas_call(functools.partial(kernel, nb, np_, tiles, blk, cl, slots),...  23.3 us
    unnamed x1, local copies, waits for them, and re-layouts  0.68 us

profile of v4, /device:TPU:5, one launch (start us, length us, event | category | flops | bytes accessed | tf_op | source)
XLA Modules:
  0.0 24.0 jit_solution(7614689837818815082)
XLA Ops:
  0.0 23.3 %decode.1 = f32[12,1,4096]{2,1,0:T(1,128)S(1)} custom-call(s32[16]{0:T(128)} %owners_in.1, s32[16,128]{1,0:T(8,128)} %rows_in.1, f32[1,512]{1,0:T(1,128)} %b1_in.1, f32[1,512]{1,0:T(1,128)} %b2_in.1, f32[1,512]{1,0:T(1,128)} %gain_in.1, bf16[12,512]{1,0:T(8,128)(2,1)} %bitcast.9, f32[1,12]{1,0:T(1,128)} %bo_in.1, bf16[2560,512]{1,0:T(8,128)(2,1)} %bitcast.6, ...), custom_call_target="tpu_custom_call" | custom-call | tf_op jit(solution)/shard_map/decode/pallas_call | solution.py:498
  23.3 0.7 %copy.13 = f32[1,12,4096]{2,0,1:T(1,128)} copy(f32[1,12,4096]{2,0,1:T(1,128)S(1)} %bitcast.5) | data formatting | bytes 393216

commit v5 on v4

--- a/solution.py
+++ b/solution.py
@@ -300,10 +300,15 @@
     pl.semaphore_wait(barrier, greetings)
     pl.when(z == 0)(lambda: share(0))
     send_pieces()
-    pl.when(z >= n_pair)(build)
-
-    @pl.when(z != 0)
+
+    @pl.when((z > 0) & (z < n_pair))
     def _():
+        front(0)
+        share(0)
+
+    @pl.when(z >= n_pair)
+    def _():
+        build()
         front(0)
         share(0)
 
@@ -414,7 +419,7 @@
 
     for k in late:
         relay(k, late[k])
-    pl.when(z != 0)(lambda: relay(0, even, other=True))
+    relay(0, even, other=True)
 
     for kk in range(tp):
         jj, i = step_of(kk)
@@ -422,7 +427,6 @@
         if kk == min(1, tb - 1):
             for k in last:
                 relay(k, last[k])
-            pl.when(z == 0)(lambda: relay(0, even, other=True))
             relay(2, even, other=True)
         tile = tile_of(kk)
         t = p * tp + tile

time: 24.2 us -> 24.2 us (level)
  no operation moved by 1% of the time
where the time goes in v5:
time: 24.2 us; the launch traced here: 24 us
  Pallas kernels  23.3 us (96%)
  local copies, waits for them, and re-layouts  0.68 us (3%)
    pallas_call x1, Pallas kernels, body(): pl.pallas_call(functools.partial(kernel, nb, np_, tiles, blk, cl, slots),...  23.3 us
    unnamed x1, local copies, waits for them, and re-layouts  0.68 us

profile of v5, /device:TPU:5, one launch (start us, length us, event | category | flops | bytes accessed | tf_op | source)
XLA Modules:
  0.0 24.0 jit_solution(15423036293570392133)
XLA Ops:
  0.0 23.3 %decode.1 = f32[12,1,4096]{2,1,0:T(1,128)S(1)} custom-call(s32[16]{0:T(128)} %owners_in.1, s32[16,128]{1,0:T(8,128)} %rows_in.1, f32[1,512]{1,0:T(1,128)} %b1_in.1, f32[1,512]{1,0:T(1,128)} %b2_in.1, f32[1,512]{1,0:T(1,128)} %gain_in.1, bf16[12,512]{1,0:T(8,128)(2,1)} %bitcast.9, f32[1,12]{1,0:T(1,128)} %bo_in.1, bf16[2560,512]{1,0:T(8,128)(2,1)} %bitcast.6, ...), custom_call_target="tpu_custom_call" | custom-call | tf_op jit(solution)/shard_map/decode/pallas_call | solution.py:502
  23.3 0.7 %copy.13 = f32[1,12,4096]{2,0,1:T(1,128)} copy(f32[1,12,4096]{2,0,1:T(1,128)S(1)} %bitcast.5) | data formatting | bytes 393216
